TPU v7x, 32 devices: a whole 2x2x4 slice. The times are simulated.
32 devices in a mesh: member: 8 (over y, x, core), tensor: 4 (over z).
Axes of the slice: x: 2, y: 2, z: 4, core: 2. Of those that a mesh axis runs over, the one named last changes fastest.
Arguments:
- prompt_acts: bfloat16 [128, 5120], P(None, 'member'), may hold values from -6 to 6
- gate_weight: bfloat16 [5120, 13824], P('member', 'tensor'), may hold values from -0.078125 to 0.078125
- up_weight: bfloat16 [5120, 13824], P('member', 'tensor'), may hold values from -0.078125 to 0.078125
- down_weight: bfloat16 [13824, 5120], P('tensor', 'member'), may hold values from -0.0546875 to 0.0546875
- d_table: bfloat16 [128, 3, 4, 5120], P('member'), may hold values from -6 to 6
- f_table: bfloat16 [128, 3, 4, 13824], P('member', None, None, 'tensor'), may hold values from -6 to 6
- seeds: int32 [64], P('member'), may hold values from 0 to 15
- fitness: float32 [64], P('member'), may hold values from -6 to 6
Outputs:
- outputs: bfloat16 [64, 128, 5120], P('member', None, 'tensor')
- delta_gate: bfloat16 [5120, 13824], P('member', 'tensor')
- delta_up: bfloat16 [5120, 13824], P('member', 'tensor')
- delta_down: bfloat16 [13824, 5120], P('tensor', 'member')
Inputs may be any that keep to these rules, and one draw needn't show every extreme that they name: Member m uses row (m // 8) * 16 + seeds[m] of both tables, a row in its own group's block.
All inputs are finite; a program needn't handle non-finite values.
Results may differ from a plain program's by a relative error of at most 0.025.
Values may be sent and summed in bfloat16 or wider, within the bound.
No kernel may reach another device: no remote copies, remote signals or barrier semaphores. Data moves between devices by JAX's collectives and lax.ppermute only.
A program may use at most 192 MiB of HBM per device.

v0:
```python
import math
import jax
import jax.numpy as jnp
from jax import lax
from jax.sharding import PartitionSpec as P

D = 5120
FFW = 13824
perturb_gain = 0.5


def shards(prompt_acts, gate_weight, up_weight, down_weight, d_table, f_table, seeds, fitness):
    members = seeds.shape[0]
    prompt_len = prompt_acts.shape[0]
    rank_size = d_table.shape[2]
    d_sel = jnp.take(d_table, seeds, axis=0)
    selected_factors = jnp.take(f_table, seeds, axis=0)
    d_slices = lax.all_to_all(d_sel, "member", split_axis=3, concat_axis=0, tiled=True)
    f_all, fit_all = (
        lax.all_gather(selected_factors, "member", axis=0, tiled=True),
        lax.all_gather(fitness.astype(jnp.bfloat16), "member", axis=0, tiled=True).astype(
            fitness.dtype
        ),
    )
    population = fit_all.shape[0]
    gate_part = jnp.dot(prompt_acts, gate_weight, preferred_element_type=jnp.float32)
    up_part = jnp.dot(prompt_acts, up_weight, preferred_element_type=jnp.float32)
    prompt_full = lax.all_gather(prompt_acts, "member", axis=1, tiled=True)
    gate_sum, up_sum = (
        lax.psum(gate_part.astype(jnp.bfloat16), "member").astype(jnp.float32),
        lax.psum(up_part.astype(jnp.bfloat16), "member").astype(jnp.float32),
    )
    in_factors = d_sel[:, :2].reshape(members * 2 * rank_size, D)
    proj_sum = jnp.dot(prompt_full, in_factors.T, preferred_element_type=jnp.float32)
    base_gate = gate_sum.astype(jnp.bfloat16)
    base_up = up_sum.astype(jnp.bfloat16)
    proj_inputs = (
        (proj_sum / math.sqrt(D)).astype(jnp.bfloat16).reshape(prompt_len, members, 2, rank_size)
    )
    perturbed = jnp.einsum(
        "pmkr,mkrf->mkpf", proj_inputs, selected_factors[:, :2], preferred_element_type=jnp.float32
    )
    gate = base_gate.astype(jnp.float32)[None] + perturb_gain * perturbed[:, 0]
    up = base_up.astype(jnp.float32)[None] + perturb_gain * perturbed[:, 1]
    hidden_state = (jax.nn.silu(gate) * up).astype(jnp.bfloat16)
    projection_here = jnp.einsum(
        "cdv,czv->cdz", hidden_state, selected_factors[:, 2], preferred_element_type=jnp.float32
    )
    proj_down = (lax.psum(projection_here, "tensor") / math.sqrt(FFW)).astype(jnp.bfloat16)
    hidden_rows = hidden_state.reshape(members * prompt_len, hidden_state.shape[2])
    partial_value = jnp.dot(
        hidden_rows,
        lax.all_gather(down_weight, "member", axis=1, tiled=True),
        preferred_element_type=jnp.float32,
    )
    summed = lax.psum_scatter(
        partial_value.astype(jnp.bfloat16), "tensor", scatter_dimension=1, tiled=True
    ).astype(jnp.float32)
    local_column_range = summed.shape[1]
    col_start = lax.axis_index("tensor") * local_column_range
    out_factor = lax.dynamic_slice_in_dim(d_sel[:, 2], col_start, local_column_range, 2)
    down_noise_delta = perturb_gain * jnp.einsum(
        "mpr,mrd->mpd", proj_down, out_factor, preferred_element_type=jnp.float32
    )
    outputs = (summed.reshape(members, prompt_len, local_column_range) + down_noise_delta).astype(
        jnp.bfloat16
    )
    mean = jnp.sum(fit_all) / population
    spread = jnp.sum((fit_all - mean) ** 2) / population
    score = (fit_all - mean) / jnp.sqrt(spread + 1.0)
    weighted = (d_slices.astype(jnp.float32) * score[:, None, None, None]).astype(jnp.bfloat16)
    scale = 1.0 / math.sqrt(population * rank_size)
    width_cols = weighted.shape[3]
    hidden_cols = f_all.shape[3]
    w_gate = weighted[:, 0].reshape(population * rank_size, width_cols)
    w_up = weighted[:, 1].reshape(population * rank_size, width_cols)
    w_down = weighted[:, 2].reshape(population * rank_size, width_cols)
    f_gate = f_all[:, 0].reshape(population * rank_size, hidden_cols)
    f_up = f_all[:, 1].reshape(population * rank_size, hidden_cols)
    down_factor_columns = f_all[:, 2].reshape(population * rank_size, hidden_cols)
    delta_gate = (jnp.dot(w_gate.T, f_gate, preferred_element_type=jnp.float32) * scale).astype(
        jnp.bfloat16
    )
    delta_up = (jnp.dot(w_up.T, f_up, preferred_element_type=jnp.float32) * scale).astype(
        jnp.bfloat16
    )
    delta_down = (
        jnp.dot(down_factor_columns.T, w_down, preferred_element_type=jnp.float32) * scale
    ).astype(jnp.bfloat16)
    return (outputs, delta_gate, delta_up, delta_down)


def solution(mesh):
    in_specs = (
        P(None, "member"),
        P("member", "tensor"),
        P("member", "tensor"),
        P("tensor", "member"),
        P("member", None, None, None),
        P("member", None, None, "tensor"),
        P("member"),
        P("member"),
    )
    out_specs = (
        P("member", None, "tensor"),
        P("member", "tensor"),
        P("member", "tensor"),
        P("tensor", "member"),
    )
    return jax.shard_map(shards, mesh=mesh, in_specs=in_specs, out_specs=out_specs, check_vma=False)
```

profile of v0, /device:TPU:0, one launch (start us, length us, event | category | flops | bytes accessed | tf_op | source)
XLA Modules:
  0.0 510.3 jit_solution(4729490581838769242)
XLA Ops:
  7.2 0.0 all-reduce.4.cloned.1.call-start
  7.2 4.3 convolution_convert_fusion.1
  11.5 4.2 convolution_convert_fusion.2
  15.6 0.0 all-reduce.4.cloned.1.call-update
  15.7 0.0 all-gather.4.cloned.1.call-start
  15.7 0.7 all-gather.4.cloned.1.call-update
  16.4 0.0 all-gather.6.cloned.1.call-start
  16.5 0.7 all-gather.6.cloned.1.call-update
  17.2 0.0 all-gather.8.cloned.1.call-start
  17.2 2.4 gather_fusion.1
  19.7 1.2 broadcast_select_fusion.1
  20.9 0.0 all-gather.8.cloned.1.call-update
  20.9 0.0 reduce-scatter.2.cloned.1.call-start
  21.0 2.3 gather_fusion
  23.3 1.8 broadcast_select_fusion
  25.1 0.2 slice.52
  25.3 1.0 reshape.64
  26.3 52.1 %all-reduce.4.cloned.1.call-done = (bf16[128,3456]{1,0:T(8,128)(2,1)}, bf16[128,3456]{1,0:T(8,128)(2,1)}) async-done(((bf16[128,3456]{1,0:T(8,128)(2,1)}, bf16[128,3456]{1,0:T(8,128)(2,1)}), (bf16[128,3456]{1,0:T(8,128)(2,1)}, bf16[128,3456]{1,0:T(8,128)(2,1)})) %all-reduce.4.cloned.1.call-update) | async-done | bytes 1769488 | tf_op jit(solution)/shard_map/psum | solution.py:31
  78.5 1.3 convert_element_type.69
  79.8 3.1 convert_element_type.73
  82.9 21.3 %all-gather.4.cloned.1.call-done = bf16[128,5120]{1,0:T(8,128)(2,1)} async-done(((bf16[128,640]{1,0:T(8,128)(2,1)}), bf16[128,5120]{1,0:T(8,128)(2,1)}) %all-gather.4.cloned.1.call-update) | async-done | bytes 1310736 | tf_op jit(solution)/shard_map/all_gather | solution.py:28
  104.2 2.1 fusion.12
  106.2 18.7 %fusion.13 = f32[8,2,128,3456]{3,2,1,0:T(8,128)} fusion(bf16[128,8,2,4]{0,3,2,1:T(4,128)(2,1)S(1)} %bitcast.104, bf16[8,3,4,3456]{3,2,1,0:T(4,128)(2,1)} %broadcast_select_fusion.1), kind=kOutput, calls=%fused_computation.34 | convolution fusion | flops 56623104 | bytes 28770304 | tf_op jit(solution)/shard_map/pmkr,mkrf->mkpf/dot_general | solution.py:40
  125.0 11.1 %fusion = f32[8,1,128,3456]{3,2,0,1:T(8,128)} fusion(f32[8,2,128,3456]{3,2,1,0:T(8,128)} %fusion.13), kind=kLoop, calls=%fused_computation.4 | loop fusion | flops 3538944 | bytes 28311552 | tf_op jit(solution)/shard_map/mul | solution.py:43
  136.1 11.2 %slice_multiply_fusion = f32[8,1,128,3456]{3,2,1,0:T(8,128)} fusion(f32[8,2,128,3456]{3,2,1,0:T(8,128)} %fusion.13), kind=kLoop, calls=%fused_computation.2 | loop fusion | flops 3538944 | bytes 28311552 | tf_op jit(solution)/shard_map/mul | solution.py:44
  147.3 13.3 %fusion.4 = bf16[1024,3456]{1,0:T(8,128)(2,1)} fusion(f32[8,1,128,3456]{3,2,1,0:T(8,128)} %slice_multiply_fusion, f32[8,1,128,3456]{3,2,0,1:T(8,128)} %fusion, f32[128,3456]{1,0:T(8,128)} %convert_element_type.73, f32[128,3456]{1,0:T(8,128)S(1)} %convert_element_type.69), kind=kLoop, calls=%fused_computation.11 | loop fusion | flops 28311552 | bytes 38928384 | tf_op jit(solution)/shard_map/convert_element_type | solution.py:45
  160.6 114.7 %all-gather.6.cloned.1.call-done = bf16[3456,5120]{1,0:T(8,128)(2,1)} async-done(((bf16[3456,640]{1,0:T(8,128)(2,1)}), bf16[3456,5120]{1,0:T(8,128)(2,1)}) %all-gather.6.cloned.1.call-update) | async-done | bytes 35389456 | tf_op jit(solution)/shard_map/all_gather | solution.py:53
  275.2 45.1 %convolution_convert_fusion = bf16[1024,5120]{1,0:T(8,128)(2,1)} fusion(bf16[1024,3456]{1,0:T(8,128)(2,1)} %fusion.4, bf16[3456,5120]{1,0:T(8,128)(2,1)} %all-gather.6.cloned.1.call-done), kind=kOutput, calls=%fused_computation.13 | convolution fusion | flops 36244029440 | bytes 52953088 | tf_op jit(solution)/shard_map/dot_general | solution.py:51
  320.4 0.0 reduce-scatter.2.cloned.1.call-update
  320.4 14.9 %copy.34 = bf16[8,3,4,5120]{0,2,1,3:T(4,128)(2,1)} copy(bf16[8,3,4,5120]{3,2,1,0:T(4,128)(2,1)S(1)} %broadcast_select_fusion) | data formatting | bytes 1966080 | tf_op jit(solution)/shard_map/jit(_take)/select_n | solution.py:16
  335.3 19.3 %reshape.104 = bf16[8,2,30720]{2,1,0:T(2,128)(2,1)} reshape(bf16[5120,3,4,8]{3,2,1,0:T(4,128)(2,1)} %bitcast.102) | data formatting | bytes 1966080
  354.6 3.6 all-to-all-start
  358.2 0.7 dynamic-slice.1
  359.5 0.2 dynamic-update-slice
  359.8 19.9 %all-reduce = bf16[64]{0:T(256)(128)(2,1)S(1)} all-reduce(bf16[64]{0:T(256)(128)(2,1)S(1)} %dynamic-update-slice), channel_id=1, replica_groups=mesh['member'=8,'tensor'=4] {'member'}, use_global_device_ids=true, to_apply=%add | all-reduce | flops 64 | bytes 256
  379.7 0.7 convert_reduce_fusion
  381.0 0.7 multiply_reduce_fusion
  382.3 19.7 %reshape.105 = bf16[5120,3,4,8]{3,2,1,0:T(4,128)(2,1)} reshape(bf16[8,2,30720]{2,1,0:T(2,128)(2,1)S(1)} %all-to-all-done) | data formatting | bytes 1966080
  402.1 19.0 %copy.35 = f32[8,3,4,8,640]{4,0,3,2,1:T(8,128)S(1)} copy(bf16[8,3,4,8,640]{0,2,1,4,3:T(4,128)(2,1)} %bitcast.101) | data formatting | bytes 2949120 | tf_op jit(solution)/shard_map/convert_element_type | solution.py:71
  421.1 0.2 fusion.11
  421.4 13.1 %fusion.8 = f32[8,128,4]{1,2,0:T(4,128)S(1)} fusion(f32[128,3456]{1,0:T(8,128)} %convert_element_type.73, f32[128,3456]{1,0:T(8,128)} %copy-done.3, bf16[8,3,4,3456]{3,2,1,0:T(4,128)(2,1)} %broadcast_select_fusion.1, f32[8,2,128,3456]{3,2,1,0:T(8,128)} %fusion.13), kind=kOutput, calls=%fused_computation.20 | convolution fusion | flops 63700992 | bytes 32088064 | tf_op jit(solution)/shard_map/cdv,czv->cdz/dot_general | solution.py:46
  434.4 20.0 %psum.23 = f32[8,128,4]{1,2,0:T(4,128)S(1)} all-reduce(f32[8,128,4]{1,2,0:T(4,128)S(1)} %fusion.8), channel_id=1, replica_groups=mesh['member'=8,'tensor'=4] {'tensor'}, use_global_device_ids=true, to_apply=%region_3.4 | all-reduce | flops 4096 | bytes 32768 | tf_op jit(solution)/shard_map/psum | solution.py:49
  454.4 3.6 fusion.23
  458.1 3.5 fusion.6
  461.5 3.5 fusion.7
  465.0 3.7 fusion.5
  468.7 30.9 %reduce-scatter.2.cloned.1.call-done = bf16[1024,1280]{1,0:T(8,128)(2,1)} async-done(((bf16[1024,5120]{1,0:T(8,128)(2,1)}), bf16[1024,1280]{1,0:T(8,128)(2,1)}) %reduce-scatter.2.cloned.1.call-update) | async-done | bytes 2621456 | tf_op jit(solution)/shard_map/reduce_scatter | solution.py:56
  499.6 4.2 fusion.10
  (24 shorter events, 0.1 us)
Async XLA Ops:
  7.2 13.8 %copy-start = (bf16[16,3,4,5120]{3,2,1,0:T(4,128)(2,1)S(1)}, bf16[16,3,4,5120]{3,2,1,0:T(4,128)(2,1)}, u32[]{:S(2)}) copy-start(bf16[16,3,4,5120]{3,2,1,0:T(4,128)(2,1)} %param.12) | copy-start | bytes 5898244
  7.2 71.3 %all-reduce.4.cloned.1.call-start = ((), (), s32[]{:S(2)}) async-start(), calls=%async_computation.6 | async-start | bytes 3538944 | tf_op jit(solution)/shard_map/psum | solution.py:31
  11.5 5.7 %copy-start.4 = (s32[8]{0:T(128)S(1)}, s32[8]{0:T(128)}, u32[]{:S(2)}) copy-start(s32[8]{0:T(128)} %param.14) | copy-start | bytes 100
  15.7 88.5 %all-gather.4.cloned.1.call-start = ((), (), s32[]{:S(2)}) async-start(), calls=%async_computation.2 | async-start | bytes 1474560 | tf_op jit(solution)/shard_map/all_gather | solution.py:28
  16.4 258.8 %all-gather.6.cloned.1.call-start = ((), (), s32[]{:S(2)}) async-start(), calls=%async_computation.3 | async-start | bytes 39813120 | tf_op jit(solution)/shard_map/all_gather | solution.py:53
  17.2 437.3 %all-gather.8.cloned.1.call-start = ((), (), s32[]{:S(2)}) async-start(), calls=%async_computation.5 | async-start | bytes 5971968 | tf_op jit(solution)/shard_map/all_gather | solution.py:20
  20.9 478.7 %reduce-scatter.2.cloned.1.call-start = ((), (), s32[]{:S(2)}) async-start(), calls=%async_computation.4 | async-start | bytes 13107200 | tf_op jit(solution)/shard_map/reduce_scatter | solution.py:56
  25.1 333.1 %copy-start.2 = (bf16[8,3,4,5120]{3,2,1,0:T(4,128)(2,1)}, bf16[8,3,4,5120]{3,2,1,0:T(4,128)(2,1)S(1)}, u32[]{:S(2)}) copy-start(bf16[8,3,4,5120]{3,2,1,0:T(4,128)(2,1)S(1)} %broadcast_select_fusion) | copy-start | bytes 2949124
  79.8 67.5 %copy-start.3 = (f32[128,3456]{1,0:T(8,128)}, f32[128,3456]{1,0:T(8,128)S(1)}, u32[]{:S(2)}) copy-start(f32[128,3456]{1,0:T(8,128)S(1)} %convert_element_type.69) | copy-start | bytes 5308420
  335.3 22.9 %copy-start.5 = (f32[8]{0:T(128)S(1)}, f32[8]{0:T(128)}, u32[]{:S(2)}) copy-start(f32[8]{0:T(128)} %param.15) | copy-start | bytes 100
  335.3 22.9 %copy-start.6 = (u32[32]{0:T(128)S(1)}, u32[32]{0:T(128)}, u32[]{:S(2)}) copy-start(u32[32]{0:T(128)} %constant.62) | copy-start | bytes 388
  354.6 27.7 %all-to-all-start = ((bf16[8,2,30720]{2,1,0:T(2,128)(2,1)}), bf16[8,2,30720]{2,1,0:T(2,128)(2,1)S(1)}, u32[]{:S(2)}, u32[]{:S(2)}) async-start(bf16[8,2,30720]{2,1,0:T(2,128)(2,1)} %reshape.104), calls=%async_computation.1 | async-start | bytes 1966080 | tf_op jit(solution)/shard_map/all_to_all | solution.py:18
  465.0 34.6 %slice-start = ((bf16[8,3,4,5120]{3,2,1,0:T(4,128)(2,1)}), bf16[8,1,4,5120]{3,2,1,0:T(4,128)(2,1)S(1)}, s32[]{:S(2)}) async-start(bf16[8,3,4,5120]{3,2,1,0:T(4,128)(2,1)} %copy-done.2), calls=%async_computation.7 | async-start | bytes 655360 | tf_op jit(solution)/shard_map/slice | solution.py:61
  465.0 38.8 %copy-start.1 = (bf16[16,3,4,5120]{3,2,1,0:T(4,128)(2,1)S(1)}, bf16[16,3,4,5120]{3,2,1,0:T(4,128)(2,1)}, u32[]{:S(2)}) copy-start(bf16[16,3,4,5120]{3,2,1,0:T(4,128)(2,1)} %param.12) | copy-start | bytes 5898244
Sparse Core Ops, SparseCore 0:
  15.8 62.6 all-reduce.3
  80.4 23.7 all-gather.3
  106.1 169.1 all-gather.5
  277.5 41.2 all-gather.7
  321.1 178.5 reduce-scatter.1
where the time goes:
time: 511 us; the launch traced here: 510 us
  waiting for transfers between devices  220 us (43%)
  matrix products  102 us (20%)
  local copies, waits for them, and re-layouts  83.5 us (16%)
  other arithmetic  44.6 us (9%)
  blocking collectives  39.9 us (8%)
  between operations  15.9 us (3%)
    all_gather x1, waiting for transfers between devices, shards(): lax.all_gather(down_weight, 'member', axis=1, tiled=True)  115 us
    psum x1, waiting for transfers between devices, shards(): lax.psum(up_part.astype(jnp.bfloat16), 'member').astype(jnp.float32)  52.1 us
    dot_general x1, matrix products, shards(): jnp.dot(hidden_rows, lax.all_gather(down_weight, 'member', axis=1, tiled=...  45.1 us
    unnamed x19, local copies, waits for them, and re-layouts  40 us
    reduce_scatter x1, waiting for transfers between devices, shards(): lax.psum_scatter(partial_value.astype(jnp.bfloat16), 'tensor', scatter_di...  30.9 us
    all_gather x1, waiting for transfers between devices, shards(): prompt_full = lax.all_gather(prompt_acts, 'member', axis=1, tiled=True)  21.3 us
    psum x1, blocking collectives, shards(): lax.psum(projection_here, 'tensor') / math.sqrt(FFW)  20 us
    unnamed x1, blocking collectives  19.9 us
  transfers between devices with their start and end apart: 6, of which 4 were waited for; matrix products, arithmetic and copies ran while one was open for 43% of the time, Pallas kernels for 0%

commit v1 on v0

--- a/solution.py
+++ b/solution.py
@@ -1,3 +1,4 @@
+import functools
 import math
 import jax
 import jax.numpy as jnp
@@ -7,6 +8,13 @@
 D = 5120
 FFW = 13824
 perturb_gain = 0.5
+
+
+def _switch_pages(inner_x, shard_axis):
+    return jnp.concatenate(lax.all_gather(inner_x, shard_axis), axis=1)
+
+
+find_sizes = functools.partial(_switch_pages, shard_axis="member")
 
 
 def shards(prompt_acts, gate_weight, up_weight, down_weight, d_table, f_table, seeds, fitness):
@@ -49,9 +57,7 @@
     proj_down = (lax.psum(projection_here, "tensor") / math.sqrt(FFW)).astype(jnp.bfloat16)
     hidden_rows = hidden_state.reshape(members * prompt_len, hidden_state.shape[2])
     partial_value = jnp.dot(
-        hidden_rows,
-        lax.all_gather(down_weight, "member", axis=1, tiled=True),
-        preferred_element_type=jnp.float32,
+        hidden_rows, find_sizes(down_weight), preferred_element_type=jnp.float32
     )
     summed = lax.psum_scatter(
         partial_value.astype(jnp.bfloat16), "tensor", scatter_dimension=1, tiled=True

time: 511 us -> 555 us (1.086)
  local copies, waits for them, and re-layouts: 83.5 us -> 128 us
  waiting for transfers between devices: 220 us -> 251 us
  other arithmetic: 44.6 us -> 21.5 us
  matrix products: 102 us -> 92.2 us
    reshape x0 -> x1, local copies, waits for them, and re-layouts: none -> 44.8 us  [_switch_pages(): return jnp.concatenate(lax.all_gather(inner_x, shard_axis), axis=1)]
    all_gather x1, waiting for transfers between devices: 115 us -> 137 us  [_switch_pages(): return jnp.concatenate(lax.all_gather(inner_x, shard_axis), axis=1)]
    mul x2 -> x0, other arithmetic: 22.2 us -> none  [the longest x1 11.2 us: shards(): up = base_up.astype(jnp.float32)[None] + perturb_gain * perturbed[:, 1]]
    dot_general x1, matrix products: 13.1 us -> 5.09 us  [shards(): jnp.einsum('cdv,czv->cdz', hidden_state, selected_factors[:, 2], preferre...]
    reduce_scatter x1, waiting for transfers between devices: 30.9 us -> 38.5 us  [shards(): lax.psum_scatter(partial_value.astype(jnp.bfloat16), 'tensor', scatter_di...]
    unnamed x19 -> x23, local copies, waits for them, and re-layouts: 40 us -> 39.9 us
  transfers between devices with their start and end apart: 6 -> 6, of which waited for: 4 -> 4; matrix products, arithmetic and copies ran while one was open for 43% -> 42% of each run, Pallas kernels for 0% -> 0%
where the time goes in v1:
time: 555 us; the launch traced here: 553 us
  waiting for transfers between devices  251 us (45%)
  local copies, waits for them, and re-layouts  128 us (23%)
  matrix products  92.2 us (17%)
  blocking collectives  40.2 us (7%)
  other arithmetic  21.5 us (4%)
  between operations  16 us (3%)
    all_gather x1, waiting for transfers between devices, _switch_pages(): return jnp.concatenate(lax.all_gather(inner_x, shard_axis), axis=1)  137 us
    psum x1, waiting for transfers between devices, shards(): lax.psum(up_part.astype(jnp.bfloat16), 'member').astype(jnp.float32)  52.1 us
    dot_general x1, matrix products, shards(): jnp.dot(hidden_rows, find_sizes(down_weight), preferred_element_type=jnp....  45.3 us
    reshape x1, local copies, waits for them, and re-layouts, _switch_pages(): return jnp.concatenate(lax.all_gather(inner_x, shard_axis), axis=1)  44.8 us
    unnamed x23, local copies, waits for them, and re-layouts  39.9 us
    reduce_scatter x1, waiting for transfers between devices, shards(): lax.psum_scatter(partial_value.astype(jnp.bfloat16), 'tensor', scatter_di...  38.5 us
    all_gather x1, waiting for transfers between devices, shards(): prompt_full = lax.all_gather(prompt_acts, 'member', axis=1, tiled=True)  21.9 us
    psum x1, blocking collectives, shards(): lax.psum(projection_here, 'tensor') / math.sqrt(FFW)  20.2 us
  transfers between devices with their start and end apart: 6, of which 4 were waited for; matrix products, arithmetic and copies ran while one was open for 42% of the time, Pallas kernels for 0%

profile of v1, /device:TPU:0, one launch (start us, length us, event | category | flops | bytes accessed | tf_op | source)
XLA Modules:
  0.0 553.1 jit_solution(14586947208636333190)
XLA Ops:
  7.2 0.0 copy-start
  7.2 0.0 all-reduce.4.cloned.1.call-start
  7.2 4.3 convolution_convert_fusion.1
  11.5 1.8 convolution_convert_fusion.2
  13.4 0.0 all-reduce.4.cloned.1.call-update
  13.4 0.0 all-gather.5.cloned.1.call-start
  13.4 0.7 all-gather.5.cloned.1.call-update
  14.1 0.0 all-gather.9.cloned.1.call-start
  14.2 0.7 all-gather.9.cloned.1.call-update
  14.9 0.0 all-gather.7.cloned.1.call-start
  15.0 2.4 gather_fusion.1
  17.4 1.2 broadcast_select_fusion.1
  18.6 0.0 all-gather.7.cloned.1.call-update
  18.6 0.0 reduce-scatter.2.cloned.1.call-start
  18.7 2.3 gather_fusion
  21.0 1.8 broadcast_select_fusion
  22.8 0.2 slice.52
  23.0 1.0 reshape.90
  24.0 52.1 %all-reduce.4.cloned.1.call-done = (bf16[128,3456]{1,0:T(8,128)(2,1)}, bf16[128,3456]{1,0:T(8,128)(2,1)}) async-done(((bf16[128,3456]{1,0:T(8,128)(2,1)}, bf16[128,3456]{1,0:T(8,128)(2,1)}), (bf16[128,3456]{1,0:T(8,128)(2,1)}, bf16[128,3456]{1,0:T(8,128)(2,1)})) %all-reduce.4.cloned.1.call-update) | async-done | bytes 1769488 | tf_op jit(solution)/shard_map/psum | solution.py:39
  76.2 1.3 convert_element_type.80
  77.5 2.5 convert_element_type.76
  80.0 21.9 %all-gather.5.cloned.1.call-done = bf16[128,5120]{1,0:T(8,128)(2,1)} async-done(((bf16[128,640]{1,0:T(8,128)(2,1)}), bf16[128,5120]{1,0:T(8,128)(2,1)}) %all-gather.5.cloned.1.call-update) | async-done | bytes 1310736 | tf_op jit(solution)/shard_map/all_gather | solution.py:36
  101.9 2.1 fusion.12
  104.0 18.9 %fusion.13 = f32[8,2,128,3456]{3,2,1,0:T(8,128)} fusion(bf16[128,8,2,4]{0,3,2,1:T(4,128)(2,1)S(1)} %bitcast.99, bf16[8,3,4,3456]{3,2,1,0:T(4,128)(2,1)} %broadcast_select_fusion.1), kind=kOutput, calls=%fused_computation.31 | convolution fusion | flops 56623104 | bytes 28770304 | tf_op jit(solution)/shard_map/pmkr,mkrf->mkpf/dot_general | solution.py:48
  122.8 13.3 %fusion.3 = bf16[8,128,3456]{2,1,0:T(8,128)(2,1)} fusion(f32[8,2,128,3456]{3,2,1,0:T(8,128)} %fusion.13, f32[128,3456]{1,0:T(8,128)S(1)} %convert_element_type.80, f32[128,3456]{1,0:T(8,128)S(1)} %copy-done.3), kind=kLoop, calls=%fused_computation.6 | loop fusion | flops 35389440 | bytes 38928384 | tf_op jit(solution)/shard_map/convert_element_type | solution.py:53
  136.1 137.3 %all-gather.9.cloned.1.call-done = bf16[27648,640]{1,0:T(8,128)(2,1)} async-done(((bf16[3456,640]{1,0:T(8,128)(2,1)}), bf16[27648,640]{1,0:T(8,128)(2,1)}) %all-gather.9.cloned.1.call-update) | async-done | bytes 35389456 | tf_op jit(solution)/shard_map/all_gather | solution.py:14
  273.4 44.8 %copy.49 = bf16[3456,8,640]{0,2,1:T(8,128)(2,1)} copy(bf16[3456,8,640]{2,0,1:T(8,128)(2,1)} %bitcast.95) | data formatting | bytes 70778880 | tf_op jit(solution)/shard_map/reshape | solution.py:14
  318.2 45.3 %convolution_convert_fusion = bf16[1024,5120]{1,0:T(8,128)(2,1)} fusion(bf16[1024,3456]{1,0:T(8,128)(2,1)} %bitcast.97, bf16[3456,5120]{0,1:T(8,128)(2,1)} %bitcast.96), kind=kOutput, calls=%fused_computation.11 | convolution fusion | flops 36244029440 | bytes 52953088 | tf_op jit(solution)/shard_map/dot_general | solution.py:59
  363.5 0.0 reduce-scatter.2.cloned.1.call-update
  363.5 14.9 %copy.50 = bf16[8,3,4,5120]{0,2,1,3:T(4,128)(2,1)} copy(bf16[8,3,4,5120]{3,2,1,0:T(4,128)(2,1)S(1)} %broadcast_select_fusion) | data formatting | bytes 1966080 | tf_op jit(solution)/shard_map/jit(_take)/select_n | solution.py:24
  378.4 19.3 %reshape.133 = bf16[8,2,30720]{2,1,0:T(2,128)(2,1)} reshape(bf16[5120,3,4,8]{3,2,1,0:T(4,128)(2,1)} %bitcast.94) | data formatting | bytes 1966080
  397.7 3.6 all-to-all-start
  401.4 0.6 dynamic-slice.1
  402.6 0.2 dynamic-update-slice
  402.9 19.9 %all-reduce = bf16[64]{0:T(256)(128)(2,1)S(1)} all-reduce(bf16[64]{0:T(256)(128)(2,1)S(1)} %dynamic-update-slice), channel_id=1, replica_groups=mesh['member'=8,'tensor'=4] {'member'}, use_global_device_ids=true, to_apply=%add | all-reduce | flops 64 | bytes 256
  422.8 0.6 convert_reduce_fusion
  424.1 0.6 multiply_reduce_fusion
  425.4 19.7 %reshape.134 = bf16[5120,3,4,8]{3,2,1,0:T(4,128)(2,1)} reshape(bf16[8,2,30720]{2,1,0:T(2,128)(2,1)S(1)} %all-to-all-done) | data formatting | bytes 1966080
  445.1 19.0 %copy.51 = f32[8,3,4,8,640]{4,0,3,2,1:T(8,128)S(1)} copy(bf16[8,3,4,8,640]{0,2,1,4,3:T(4,128)(2,1)} %bitcast.93) | data formatting | bytes 2949120 | tf_op jit(solution)/shard_map/convert_element_type | solution.py:77
  464.1 0.2 fusion.11
  464.4 5.1 fusion.15
  469.5 20.2 %psum.23 = f32[8,128,4]{1,2,0:T(4,128)S(1)} all-reduce(f32[8,128,4]{1,2,0:T(4,128)S(1)} %fusion.15), channel_id=1, replica_groups=mesh['member'=8,'tensor'=4] {'tensor'}, use_global_device_ids=true, to_apply=%region_3.4 | all-reduce | flops 4096 | bytes 32768 | tf_op jit(solution)/shard_map/psum | solution.py:57
  489.7 3.6 fusion.22
  493.3 3.5 fusion.9
  496.8 3.5 fusion.8
  500.3 3.7 fusion.7
  504.0 38.5 %reduce-scatter.2.cloned.1.call-done = bf16[1024,1280]{1,0:T(8,128)(2,1)} async-done(((bf16[1024,5120]{1,0:T(8,128)(2,1)}), bf16[1024,1280]{1,0:T(8,128)(2,1)}) %reduce-scatter.2.cloned.1.call-update) | async-done | bytes 2621456 | tf_op jit(solution)/shard_map/reduce_scatter | solution.py:62
  542.5 4.2 fusion.10
  (27 shorter events, 0.1 us)
Async XLA Ops:
  7.2 11.5 %copy-start = (bf16[16,3,4,5120]{3,2,1,0:T(4,128)(2,1)S(1)}, bf16[16,3,4,5120]{3,2,1,0:T(4,128)(2,1)}, u32[]{:S(2)}) copy-start(bf16[16,3,4,5120]{3,2,1,0:T(4,128)(2,1)} %param.12) | copy-start | bytes 5898244
  7.2 4.3 copy-start.5
  7.2 69.0 %all-reduce.4.cloned.1.call-start = ((), (), s32[]{:S(2)}) async-start(), calls=%async_computation.6 | async-start | bytes 3538944 | tf_op jit(solution)/shard_map/psum | solution.py:39
  7.2 4.3 copy-start.4
  13.4 1.6 copy-start.6
  13.4 88.5 %all-gather.5.cloned.1.call-start = ((), (), s32[]{:S(2)}) async-start(), calls=%async_computation.2 | async-start | bytes 1474560 | tf_op jit(solution)/shard_map/all_gather | solution.py:36
  14.1 259.3 %all-gather.9.cloned.1.call-start = ((), (), s32[]{:S(2)}) async-start(), calls=%async_computation.5 | async-start | bytes 39813120 | tf_op jit(solution)/shard_map/all_gather | solution.py:14
  14.9 474.8 %all-gather.7.cloned.1.call-start = ((), (), s32[]{:S(2)}) async-start(), calls=%async_computation.4 | async-start | bytes 5971968 | tf_op jit(solution)/shard_map/all_gather | solution.py:28
  18.6 523.8 %reduce-scatter.2.cloned.1.call-start = ((), (), s32[]{:S(2)}) async-start(), calls=%async_computation.3 | async-start | bytes 13107200 | tf_op jit(solution)/shard_map/reduce_scatter | solution.py:62
  22.8 378.5 %copy-start.2 = (bf16[8,3,4,5120]{3,2,1,0:T(4,128)(2,1)}, bf16[8,3,4,5120]{3,2,1,0:T(4,128)(2,1)S(1)}, u32[]{:S(2)}) copy-start(bf16[8,3,4,5120]{3,2,1,0:T(4,128)(2,1)S(1)} %broadcast_select_fusion) | copy-start | bytes 2949124
  104.0 18.9 %copy-start.3 = (f32[128,3456]{1,0:T(8,128)S(1)}, f32[128,3456]{1,0:T(8,128)}, u32[]{:S(2)}) copy-start(f32[128,3456]{1,0:T(8,128)} %convert_element_type.76) | copy-start | bytes 5308420
  378.4 22.9 %copy-start.7 = (f32[8]{0:T(128)S(1)}, f32[8]{0:T(128)}, u32[]{:S(2)}) copy-start(f32[8]{0:T(128)} %param.15) | copy-start | bytes 100
  378.4 22.9 %copy-start.8 = (u32[32]{0:T(128)S(1)}, u32[32]{0:T(128)}, u32[]{:S(2)}) copy-start(u32[32]{0:T(128)} %constant.62) | copy-start | bytes 388
  397.7 27.6 %all-to-all-start = ((bf16[8,2,30720]{2,1,0:T(2,128)(2,1)}), bf16[8,2,30720]{2,1,0:T(2,128)(2,1)S(1)}, u32[]{:S(2)}, u32[]{:S(2)}) async-start(bf16[8,2,30720]{2,1,0:T(2,128)(2,1)} %reshape.133), calls=%async_computation.1 | async-start | bytes 1966080 | tf_op jit(solution)/shard_map/all_to_all | solution.py:26
  500.3 42.2 %slice-start = ((bf16[8,3,4,5120]{3,2,1,0:T(4,128)(2,1)}), bf16[8,1,4,5120]{3,2,1,0:T(4,128)(2,1)S(1)}, s32[]{:S(2)}) async-start(bf16[8,3,4,5120]{3,2,1,0:T(4,128)(2,1)} %copy-done.2), calls=%async_computation.7 | async-start | bytes 655360 | tf_op jit(solution)/shard_map/slice | solution.py:67
  500.3 46.3 %copy-start.1 = (bf16[16,3,4,5120]{3,2,1,0:T(4,128)(2,1)S(1)}, bf16[16,3,4,5120]{3,2,1,0:T(4,128)(2,1)}, u32[]{:S(2)}) copy-start(bf16[16,3,4,5120]{3,2,1,0:T(4,128)(2,1)} %param.12) | copy-start | bytes 5898244
Sparse Core Ops, SparseCore 0:
  13.5 62.6 all-reduce.3
  78.1 23.7 all-gather.4
  103.8 169.5 all-gather.8
  275.7 41.2 all-gather.6
  363.6 178.7 reduce-scatter.1
